TPU v7x, 32 devices: a whole 2x2x4 slice. The times are simulated.
32 devices in a mesh: dp: 2 (over x), tp: 16 (over z, y, core).
Axes of the slice: x: 2, y: 2, z: 4, core: 2. Of those that a mesh axis runs over, the one named last changes fastest.
Arguments:
- x_in: bfloat16 [1024, 7168], P('dp'), parts along dimension 0
- pos_ids: int32 [1024], P('dp'), parts along dimension 0
- ckv_cache: bfloat16 [2, 1024, 256, 512], P(None, 'dp'), parts along dimension 1
- kpe_cache: bfloat16 [2, 1024, 256, 64], P(None, 'dp'), parts along dimension 1
- attn_gain: bfloat16 [2, 7168], replicated
- w_dq: bfloat16 [2, 7168, 1536], replicated
- q_gain: bfloat16 [2, 1536], replicated
- w_dkv: bfloat16 [2, 7168, 576], replicated
- kv_gain: bfloat16 [2, 512], replicated
- w_uq: bfloat16 [2, 1536, 64, 192], P(None, None, 'tp')
- w_uk: bfloat16 [2, 512, 64, 128], P(None, None, 'tp')
- w_uv: bfloat16 [2, 512, 64, 128], P(None, None, 'tp')
- w_o: bfloat16 [2, 64, 128, 7168], P(None, 'tp')
- mlp_gain: bfloat16 [2, 7168], replicated
- w_gate: bfloat16 [2, 7168, 4608], P(None, None, 'tp')
- w_up: bfloat16 [2, 7168, 4608], P(None, None, 'tp')
- w_down: bfloat16 [2, 4608, 7168], P(None, 'tp')
Outputs:
- output 1: bfloat16 [1024, 7168], P('dp'), parts along dimension 0
- output 2: bfloat16 [2, 1024, 512], P(None, 'dp'), parts along dimension 1
- output 3: bfloat16 [2, 1024, 64], P(None, 'dp'), parts along dimension 1
There are 2 independent parts. A program takes and returns all parts, laid end to end along the dimension named above; an argument that names none is the same for every part.
All inputs are finite; a program needn't handle non-finite values.
Results may differ from a plain program's by a relative error of at most 0.02.
Values are sent between devices in bfloat16 or wider.
A program may use at most 1.75 GiB of HBM per device.

v0:
```python
import functools
import math
import jax
import jax.numpy as jnp
from jax import lax
from jax.experimental import pallas as pl
from jax.experimental.pallas import tpu as pltpu
from jax.sharding import PartitionSpec as P

NORM_EPS = 1e-6
ROPE_BASE = 10000.0
MESH = pl.DeviceIdType.MESH
RING = 8
CHUNK = 32
PIECE = 16
HALF = 256


def rms_norm(values, norm_gain):
    values = values.astype(jnp.float32)
    inv_rms = lax.rsqrt(jnp.mean(values * values, axis=-1, keepdims=True) + NORM_EPS)
    return (values * inv_rms * norm_gain.astype(jnp.float32)).astype(jnp.bfloat16)


def rotary(values, positions):
    half_dim = values.shape[-1] // 2
    inv_freq = jnp.exp(jnp.arange(half_dim, dtype=jnp.float32) * (-2.0 * math.log(ROPE_BASE) / values.shape[-1]))
    angles = positions.astype(jnp.float32)[..., None] * inv_freq
    cos_part = jnp.cos(angles)
    sin_part = jnp.sin(angles)
    lo_half = values[..., :half_dim]
    hi_half = values[..., half_dim:]
    return jnp.concatenate([lo_half * cos_part - hi_half * sin_part, hi_half * cos_part + lo_half * sin_part], axis=-1)


def ring_place():
    index = lax.axis_index('tp')
    core = index % 2
    chip = index // 2
    y = chip % 2
    z = chip // 2
    return core, z * (1 - y) + (7 - z) * y


def ring_device(position, core):
    y = position // 4
    z = position * (1 - y) + (7 - position) * y
    return (z * 2 + y) * 2 + core


def comm_kernel(reduce, norm, gather, canonical, subs, *refs):
    refs = list(refs)
    if reduce:
        part_ref = refs.pop(0)
        hidden_ref = refs.pop(0)
        gain_ref = refs.pop(0) if norm else None
        state_ref = refs.pop(0) if norm else None
        normed_ref = refs.pop(0) if norm and not gather else None
    else:
        shard_ref = refs.pop(0)
    full_ref = refs.pop(0) if gather else None
    if reduce:
        pair_buf, recv_buf, send_buf, pair_send, pair_recv, rs_send, rs_recv = refs[:7]
        refs = refs[7:]
    if gather:
        ag_send, ag_recv, fw_send, fw_recv = refs[:4]
    core, me = ring_place()
    dp_index = lax.axis_index('dp')
    right = (dp_index, ring_device((me + 1) % RING, core))
    left = (dp_index, ring_device((me + RING - 1) % RING, core))
    peer = (dp_index, ring_device(me, 1 - core))
    width = (part_ref if reduce else shard_ref).shape[-1]
    cols = width // subs

    barrier = pltpu.get_barrier_semaphore()
    for other in (left, right, peer):
        pl.semaphore_signal(barrier, inc=1, device_id=other, device_id_type=MESH)
    pl.semaphore_wait(barrier, 3)

    def remote(src, dst, send, recv, target):
        copy = pltpu.make_async_remote_copy(src_ref=src, dst_ref=dst, send_sem=send, recv_sem=recv, device_id=target, device_id_type=MESH)
        copy.start()
        return copy

    pending = []
    ways = ((right, -1), (left, 1))
    if reduce:
        pair_copies = {}
        for step in range(RING):
            for way, (target, sign) in enumerate(ways):
                piece = step * 2 + way
                chunk = (me + RING + sign * (1 + step)) % RING
                row = pl.multiple_of(chunk * CHUNK + way * PIECE, PIECE)
                pair_copies[piece] = remote(part_ref.at[pl.ds(HALF + row, PIECE)], pair_buf.at[piece], pair_send.at[piece], pair_recv.at[piece], peer)
        ring_copies = {}
        for step in range(RING):
            for way, (target, sign) in enumerate(ways):
                piece = step * 2 + way
                chunk = (me + RING + sign * (1 + step)) % RING
                row = pl.multiple_of(chunk * CHUNK + way * PIECE, PIECE)
                pair_copies[piece].wait()
                for sub in range(subs):
                    span = pl.ds(sub * cols, cols)
                    total = part_ref[pl.ds(row, PIECE), span].astype(jnp.float32) + pair_buf[piece, :, span].astype(jnp.float32)
                    if step > 0:
                        before = ring_copies[step - 1, way, sub]
                        before.wait_recv()
                        pending.append(before)
                        total = total + recv_buf[(step - 1) * 2 + way, :, span].astype(jnp.float32)
                    if step < RING - 1:
                        send_buf[piece, :, span] = total.astype(jnp.bfloat16)
                        ring_copies[step, way, sub] = remote(send_buf.at[piece, :, span], recv_buf.at[piece, :, span], rs_send.at[piece * subs + sub], rs_recv.at[piece * subs + sub], target)
                    else:
                        rows = pl.ds(way * PIECE, PIECE)
                        mixed = (hidden_ref[rows, span].astype(jnp.float32) + total).astype(jnp.bfloat16)
                        if norm:
                            state_ref[rows, span] = mixed
                        else:
                            own = pl.multiple_of((core * HALF if canonical else 0) + me * CHUNK + way * PIECE, PIECE)
                            full_ref[pl.ds(own, PIECE), span] = mixed
        if norm:
            for way in range(2):
                rows = pl.ds(way * PIECE, PIECE)
                values = state_ref[rows, :].astype(jnp.float32)
                inv_rms = lax.rsqrt(jnp.mean(values * values, axis=-1, keepdims=True) + NORM_EPS)
                normed = (values * inv_rms * gain_ref[...].astype(jnp.float32)).astype(jnp.bfloat16)
                if gather:
                    own = pl.multiple_of((core * HALF if canonical else 0) + me * CHUNK + way * PIECE, PIECE)
                    full_ref[pl.ds(own, PIECE), :] = normed
                else:
                    normed_ref[rows, :] = normed
    elif gather:
        own = pl.multiple_of((core * HALF if canonical else 0) + me * CHUNK, PIECE)
        full_ref[pl.ds(own, CHUNK), :] = shard_ref[...]
    if gather:
        base_here = core * HALF if canonical else 0
        base_peer = core * HALF if canonical else HALF

        def place(base, chunk, way):
            return pl.ds(pl.multiple_of(base + chunk * CHUNK + way * PIECE, PIECE), PIECE)

        ring_copies = {}
        fw_copies = []
        for step in range(RING):
            for way, (target, sign) in enumerate(ways):
                chunk = (me + RING + sign * step) % RING
                here = place(base_here, chunk, way)
                there = place(base_peer, chunk, way)
                for sub in range(subs):
                    span = pl.ds(sub * cols, cols)
                    slot = (step * 2 + way) * subs + sub
                    if step > 0:
                        before = ring_copies[step - 1, way, sub]
                        before.wait_recv()
                        pending.append(before)
                    if step < RING - 1:
                        ring_copies[step, way, sub] = remote(full_ref.at[here, span], full_ref.at[here, span], ag_send.at[slot], ag_recv.at[slot], target)
                    fw_copies.append(remote(full_ref.at[here, span], full_ref.at[there, span], fw_send.at[slot], fw_recv.at[slot], peer))
        for copy in fw_copies:
            copy.wait()
    for copy in pending:
        copy.wait_send()


def comm_call(call_id, reduce, norm, gather, canonical, subs, operands, width):
    vmem = pl.BlockSpec(memory_space=pltpu.VMEM)
    outs = []
    if reduce and norm:
        outs.append(jax.ShapeDtypeStruct((CHUNK, width), jnp.bfloat16))
        if not gather:
            outs.append(jax.ShapeDtypeStruct((CHUNK, width), jnp.bfloat16))
    if gather:
        outs.append(jax.ShapeDtypeStruct((2 * HALF, width), jnp.bfloat16))
    scratch = []
    dma = pltpu.SemaphoreType.DMA
    if reduce:
        scratch += [pltpu.VMEM((16, PIECE, width), jnp.bfloat16), pltpu.VMEM((14, PIECE, width), jnp.bfloat16), pltpu.VMEM((14, PIECE, width), jnp.bfloat16)]
        scratch += [dma((16,)), dma((16,)), dma((14 * subs,)), dma((14 * subs,))]
    if gather:
        scratch += [dma((14 * subs,)), dma((14 * subs,)), dma((16 * subs,)), dma((16 * subs,))]
    return pl.pallas_call(
        functools.partial(comm_kernel, reduce, norm, gather, canonical, subs),
        out_shape=outs,
        in_specs=[vmem] * len(operands),
        out_specs=[vmem] * len(outs),
        scratch_shapes=scratch,
        compiler_params=pltpu.CompilerParams(collective_id=call_id, has_side_effects=True, vmem_limit_bytes=48 * 1024 * 1024),
        name='comm%d' % call_id,
    )(*operands)


def layer_kernel(layer, last, subs, scale, *refs):
    refs = list(refs)
    pos_ref, q_ref, r_ref, cnew_ref, knew_ref, wuv_ref, hidden_ref, gain_ref = refs[:8]
    refs = refs[8:]
    next_ref = None if last else refs.pop(0)
    ckv_hbm, kpe_hbm, wo_hbm, gate_hbm, up_hbm, down_hbm = refs[:6]
    refs = refs[6:]
    if last:
        full_ref = b_full = refs.pop(0)
    else:
        state_out, normed_out, b_full = refs[:3]
        refs = refs[3:]
    (ckv, kpe, o_own, o_out, o_in, wo, gate, up, down, batch, act, state, own_part, pair_out, pair_buf, recv_buf, send_buf,
     ckv_sem, kpe_sem, o_send, o_recv, w_sem, pair_send, pair_recv, rs_send, rs_recv, ag_send, ag_recv, fw_send, fw_recv) = refs
    width = hidden_ref.shape[-1]
    cols = width // subs
    block = 1024
    blocks = width // block
    ffn = gate.shape[0]
    core, me = ring_place()
    dp_index = lax.axis_index('dp')
    right = (dp_index, ring_device((me + 1) % RING, core))
    left = (dp_index, ring_device((me + RING - 1) % RING, core))
    peer = (dp_index, ring_device(me, 1 - core))
    ways = ((right, -1), (left, 1))

    def wo_copy(i):
        span = pl.ds(pl.multiple_of(i * block, block), block)
        return pltpu.make_async_copy(wo_hbm.at[layer, :, span], wo.at[:, span], w_sem.at[i])

    gate_copy = pltpu.make_async_copy(gate_hbm.at[layer], gate, w_sem.at[blocks])
    up_copy = pltpu.make_async_copy(up_hbm.at[layer], up, w_sem.at[blocks + 1])
    down_copy = pltpu.make_async_copy(down_hbm.at[layer], down.at[pl.ds(0, ffn)], w_sem.at[blocks + 2])
    seqs = ckv.shape[1]
    quarters = CHUNK // seqs

    def seq_row(step, k):
        way, part = divmod(k, quarters // 2)
        return pl.multiple_of(piece_row(step + 1, way) + part * seqs, seqs)

    def cache_copies(step, k):
        at = pl.ds(pl.multiple_of(core * HALF + seq_row(step, k), seqs), seqs)
        return (pltpu.make_async_copy(ckv_hbm.at[layer, at], ckv.at[k], ckv_sem.at[k]), pltpu.make_async_copy(kpe_hbm.at[layer, at], kpe.at[k], kpe_sem.at[k]))

    def piece_row(step, way):
        chunk = (me + RING + (step if way else -step)) % RING
        return pl.multiple_of(chunk * CHUNK + way * PIECE, PIECE)

    for k in range(quarters):
        for copy in cache_copies(0, k):
            copy.start()
    for i in range(blocks):
        wo_copy(i).start()
    gate_copy.start()
    up_copy.start()
    down_copy.start()

    barrier = pltpu.get_barrier_semaphore()
    for other in (left, right, peer):
        pl.semaphore_signal(barrier, inc=1, device_id=other, device_id_type=MESH)
    pl.semaphore_wait(barrier, 3)

    def remote(src, dst, send, recv, target):
        return pltpu.make_async_remote_copy(src_ref=src, dst_ref=dst, send_sem=send, recv_sem=recv, device_id=target, device_id_type=MESH)

    def o_copy(step):
        return remote(o_out.at[step], o_in.at[step], o_send.at[step], o_recv.at[step], peer)

    def attend(step):
        heads, steps = q_ref.shape[1], ckv.shape[2]
        value = wuv_ref.shape[1] // heads
        mine = o_own.shape[-1]
        key_steps = lax.broadcasted_iota(jnp.int32, (heads, steps), 1)
        row_head = lax.broadcasted_iota(jnp.int32, (seqs, heads, wuv_ref.shape[1]), 1)
        col_head = lax.broadcasted_iota(jnp.int32, (seqs, heads, wuv_ref.shape[1]), 2) // value

        def score(k):
            row = seq_row(step, k)
            for copy in cache_copies(step, k):
                copy.wait()
            scores = []
            for j in range(seqs):
                s = lax.dot_general(q_ref[row + j], ckv[k, j], (((1,), (1,)), ((), ())), preferred_element_type=jnp.float32)
                scores.append(s + jnp.dot(r_ref[row + j], kpe[k, j], preferred_element_type=jnp.float32))
            return scores

        def weigh(k, scores):
            row = seq_row(step, k)
            c_new = cnew_ref[pl.ds(row, seqs), :].astype(jnp.float32)
            k_new = knew_ref[pl.ds(row, seqs), :].astype(jnp.float32)
            context = []
            for j in range(seqs):
                pos = pos_ref[core * HALF + row + j]
                fresh = jnp.sum(q_ref[row + j].astype(jnp.float32) * c_new[j:j + 1], axis=-1, keepdims=True)
                fresh = fresh + jnp.sum(r_ref[row + j].astype(jnp.float32) * k_new[j:j + 1], axis=-1, keepdims=True)
                at_pos = key_steps == pos
                s = jnp.where(at_pos, fresh, scores[j]) * scale
                s = jnp.where(key_steps <= pos, s, -jnp.inf)
                e = jnp.exp(s - jnp.max(s, axis=-1, keepdims=True))
                p = (e / jnp.sum(e, axis=-1, keepdims=True)).astype(jnp.bfloat16).astype(jnp.float32)
                fresh_prob = jnp.sum(jnp.where(at_pos, p, 0.0), axis=-1, keepdims=True)
                c = jnp.dot(jnp.where(at_pos, 0.0, p).astype(jnp.bfloat16), ckv[k, j], preferred_element_type=jnp.float32)
                context.append((c + fresh_prob * c_new[j:j + 1]).astype(jnp.bfloat16))
            spread = jnp.dot(jnp.concatenate(context, axis=0), wuv_ref[...], preferred_element_type=jnp.float32)
            spread = spread.reshape(seqs, heads, wuv_ref.shape[1])
            out = jnp.sum(jnp.where(row_head == col_head, spread, 0.0), axis=1).astype(jnp.bfloat16)
            o_own[step, pl.ds(k * seqs, seqs), :] = out[:, :mine]
            o_out[step, pl.ds(k * seqs, seqs), :] = out[:, mine:]
            for copy in cache_copies((step + 1) % RING, k):
                copy.start()

        scores = score(0)
        for k in range(quarters):
            later = score(k + 1) if k + 1 < quarters else None
            weigh(k, scores)
            scores = later
        o_copy(step).start()

    def pair_copy(step):
        return remote(pair_out.at[step], pair_buf.at[step], pair_send.at[step], pair_recv.at[step], peer)

    def rs_copy(step, way, sub):
        slot = (step * 2 + way) * subs + sub
        where = (step, pl.ds(way * PIECE, PIECE), pl.ds(sub * cols, cols))
        return remote(send_buf.at[where], recv_buf.at[where], rs_send.at[slot], rs_recv.at[slot], ways[way][0])

    def reduce_scatter(attention, weight, ready, finish):
        def multiply(step):
            if attention:
                o_copy(step).wait_recv()
                lhs = jnp.concatenate([o_own[step], o_in[step]], axis=0)
            else:
                near, far = piece_row(step + 1, 0), piece_row(step + 1, 1)
                lhs = jnp.concatenate([act[pl.ds(pl.multiple_of(base + at, PIECE), PIECE), :] for base in (0, HALF) for at in (near, far)], axis=0)

            def one_block(i, carry):
                span = pl.ds(pl.multiple_of(i * block, block), block)
                if ready is not None:
                    @pl.when(step == 0)
                    def _():
                        ready(i)
                prod = jnp.dot(lhs, weight[:, span], preferred_element_type=jnp.float32)
                own_part[step % 2, :, span] = prod[:CHUNK]
                pair_out[step, :, span] = prod[CHUNK:].astype(jnp.bfloat16)
                return carry

            lax.fori_loop(0, blocks, one_block, 0)
            pair_copy(step).start()

        def pass_on(step):
            pair_copy(step).wait_recv()
            for sub in range(subs):
                span = pl.ds(sub * cols, cols)
                for way in range(2):
                    rows = pl.ds(way * PIECE, PIECE)

                    @pl.when(step > 0)
                    def _():
                        rs_copy(step - 1, way, sub).wait_recv()
                        own_part[step % 2, rows, span] += recv_buf[step - 1, rows, span].astype(jnp.float32)

                    total = own_part[step % 2, rows, span] + pair_buf[step, rows, span].astype(jnp.float32)

                    @pl.when(step < RING - 1)
                    def _():
                        send_buf[step, rows, span] = total.astype(jnp.bfloat16)
                        rs_copy(step, way, sub).start()

                    @pl.when(step == RING - 1)
                    def _():
                        finish(rows, span, total)

        def staggered(i, carry):
            if attention:
                @pl.when(i < RING)
                def _():
                    attend(i)

                @pl.when(i > 1)
                def _():
                    pass_on(i - 2)

                @pl.when((i > 0) & (i <= RING))
                def _():
                    multiply(i - 1)
            else:
                @pl.when(i < RING)
                def _():
                    multiply(i)

                @pl.when(i > 0)
                def _():
                    pass_on(i - 1)
            return carry

        lax.fori_loop(0, RING + (2 if attention else 1), staggered, 0)
        if attention:
            for k in range(quarters):
                for copy in cache_copies(0, k):
                    copy.wait()

        def drain(step, carry):
            pair_copy(step).wait_send()
            if attention:
                o_copy(step).wait_send()

            @pl.when(step < RING - 1)
            def _():
                for way in range(2):
                    for sub in range(subs):
                        rs_copy(step, way, sub).wait_send()
            return carry

        lax.fori_loop(0, RING, drain, 0)

    def normalise(values, gain):
        values = values.astype(jnp.float32)
        inv_rms = lax.rsqrt(jnp.mean(values * values, axis=-1, keepdims=True) + NORM_EPS)
        return (values * inv_rms * gain[...].astype(jnp.float32)).astype(jnp.bfloat16)

    def all_gather(buf, base_here, base_there, consume):
        def ag_copy(step, way, sub):
            slot = (step * 2 + way) * subs + sub
            here = buf.at[pl.ds(pl.multiple_of(base_here + piece_row(step, way), PIECE), PIECE), pl.ds(sub * cols, cols)]
            return remote(here, here, ag_send.at[slot], ag_recv.at[slot], ways[way][0])

        def fw_copy(step, way, sub):
            slot = (step * 2 + way) * subs + sub
            here = buf.at[pl.ds(pl.multiple_of(base_here + piece_row(step, way), PIECE), PIECE), pl.ds(sub * cols, cols)]
            there = buf.at[pl.ds(pl.multiple_of(base_there + piece_row(step, way), PIECE), PIECE), pl.ds(sub * cols, cols)]
            return remote(here, there, fw_send.at[slot], fw_recv.at[slot], peer)

        def two_steps(pair, carry):
            for odd in range(2):
                step = pair * 2 + odd
                for sub in range(subs):
                    for way in range(2):
                        if odd:
                            ag_copy(step - 1, way, sub).wait_recv()
                        else:
                            @pl.when(pair > 0)
                            def _():
                                ag_copy(step - 1, way, sub).wait_recv()
                        if odd:
                            @pl.when(pair < RING // 2 - 1)
                            def _():
                                ag_copy(step, way, sub).start()
                        else:
                            ag_copy(step, way, sub).start()
                        fw_copy(step, way, sub).start()
            for odd in range(2):
                for way in range(2):
                    for sub in range(subs):
                        fw_copy(pair * 2 + odd, way, sub).wait_recv()
            if consume is not None:
                consume(pair)
            return carry

        lax.fori_loop(0, RING // 2, two_steps, 0)

        def drain(step, carry):
            for way in range(2):
                for sub in range(subs):
                    fw_copy(step, way, sub).wait_send()

                    @pl.when(step < RING - 1)
                    def _():
                        ag_copy(step, way, sub).wait_send()
            return carry

        lax.fori_loop(0, RING, drain, 0)

    def finish_mid(rows, span, total):
        state[rows, span] = (hidden_ref[rows, span].astype(jnp.float32) + total).astype(jnp.bfloat16)

    reduce_scatter(True, wo, lambda i: wo_copy(i).wait(), finish_mid)
    b_full[pl.ds(pl.multiple_of(me * CHUNK, CHUNK), CHUNK), :] = normalise(state[...], gain_ref)
    down[pl.ds(ffn, down.shape[0] - ffn), :] = jnp.zeros((down.shape[0] - ffn, width), jnp.bfloat16)
    gate_copy.wait()
    up_copy.wait()
    down_copy.wait()

    def mlp_rows(pair):
        places = [(base, step, way) for base in (0, HALF) for step in range(2) for way in range(2)]
        for i, (base, odd, way) in enumerate(places):
            at = pl.multiple_of(base + piece_row(pair * 2 + odd, way), PIECE)
            batch[pl.ds(i * PIECE, PIECE), :] = b_full[pl.ds(at, PIECE), :]
        dims = (((1,), (1,)), ((), ()))
        gate_pre = lax.dot_general(gate[...], batch[...], dims, preferred_element_type=jnp.float32)
        up_pre = lax.dot_general(up[...], batch[...], dims, preferred_element_type=jnp.float32)
        hidden_act = jax.nn.silu(gate_pre) * up_pre
        padded = jnp.concatenate([hidden_act, jnp.zeros((act.shape[1] - ffn, 128), jnp.float32)], axis=0)
        turned = jnp.transpose(padded).astype(jnp.bfloat16)
        for i, (base, odd, way) in enumerate(places):
            at = pl.multiple_of(base + piece_row(pair * 2 + odd, way), PIECE)
            act[pl.ds(at, PIECE), :] = turned[i * PIECE:(i + 1) * PIECE]

    all_gather(b_full, 0, HALF, mlp_rows)

    def finish_out(rows, span, total):
        mixed = (state[rows, span].astype(jnp.float32) + total).astype(jnp.bfloat16)
        if last:
            own = pl.multiple_of(core * HALF + me * CHUNK + rows.start, PIECE)
            full_ref[pl.ds(own, PIECE), span] = mixed
        else:
            state_out[rows, span] = mixed

    reduce_scatter(False, down, None, finish_out)
    if last:
        all_gather(full_ref, core * HALF, core * HALF, None)
    else:
        normed_out[...] = normalise(state_out[...], next_ref)


def layer_call(call_id, layer, last, positions, q_lat, q_rope, c_new, k_new, w_uv, ckv_cache, kpe_cache, state, gain, next_gain, w_o, gate_t, up_t, w_down, scale):
    subs = 4
    seqs = 8
    width = state.shape[-1]
    ffn = gate_t.shape[1]
    padded = 384
    vmem = pl.BlockSpec(memory_space=pltpu.VMEM)
    hbm = pl.BlockSpec(memory_space=pl.ANY)
    small = [q_lat, q_rope, c_new, k_new, w_uv, state, gain] + ([] if last else [next_gain])
    shard = jax.ShapeDtypeStruct((CHUNK, width), jnp.bfloat16)
    outs = [jax.ShapeDtypeStruct((2 * HALF, width), jnp.bfloat16)] if last else [shard, shard]
    bf = lambda *shape: pltpu.VMEM(shape, jnp.bfloat16)
    dma = pltpu.SemaphoreType.DMA
    quarters = CHUNK // seqs
    mine = w_o.shape[1]
    scratch = ([] if last else [bf(2 * HALF, width)]) + [
        bf(quarters, seqs, *ckv_cache.shape[2:]), bf(quarters, seqs, *kpe_cache.shape[2:]), bf(RING, CHUNK, mine), bf(RING, CHUNK, mine), bf(RING, CHUNK, mine),
        bf(mine, width), bf(ffn, width), bf(ffn, width), bf(padded, width), bf(128, width), bf(2 * HALF, padded),
        bf(CHUNK, width), pltpu.VMEM((2, CHUNK, width), jnp.float32), bf(RING, CHUNK, width), bf(RING, CHUNK, width), bf(RING - 1, CHUNK, width), bf(RING - 1, CHUNK, width),
        dma((quarters,)), dma((quarters,)), dma((RING,)), dma((RING,)), dma((10,)), dma((RING,)), dma((RING,)),
        dma((14 * subs,)), dma((14 * subs,)), dma((14 * subs,)), dma((14 * subs,)), dma((16 * subs,)), dma((16 * subs,))]
    return pl.pallas_call(
        functools.partial(layer_kernel, layer, last, subs, scale),
        out_shape=outs,
        in_specs=[pl.BlockSpec(memory_space=pltpu.SMEM)] + [vmem] * len(small) + [hbm] * 6,
        out_specs=[vmem] * len(outs),
        scratch_shapes=scratch,
        compiler_params=pltpu.CompilerParams(collective_id=call_id, has_side_effects=True, vmem_limit_bytes=67043328),
        name='layer%d' % layer,
    )(positions, *small, ckv_cache, kpe_cache, w_o, gate_t, up_t, w_down)


def query_kernel(c_ref, cos_ref, sin_ref, own_q, peer_q, wk_ref, u_ref, r_ref):
    both_last = (((1,), (1,)), ((), ()))
    nope = wk_ref.shape[2]
    half = cos_ref.shape[1]
    for group, weight in enumerate((own_q, peer_q)):
        for h in range(weight.shape[1]):
            head = group * weight.shape[1] + h
            q = lax.dot_general(c_ref[...], weight[0, h], both_last, preferred_element_type=jnp.float32)
            lo, hi = q[:, nope:nope + half], q[:, nope + half:]
            r_ref[head] = jnp.concatenate([lo * cos_ref[...] - hi * sin_ref[...], hi * cos_ref[...] + lo * sin_ref[...]], axis=-1).astype(jnp.bfloat16)
            u_ref[head] = lax.dot_general(q[:, :nope].astype(jnp.bfloat16), wk_ref[head], both_last, preferred_element_type=jnp.float32).astype(jnp.bfloat16)


def query_call(layer, c_q, cos_part, sin_part, own_q, peer_q, w_k):
    rows = c_q.shape[0]
    heads, latent = w_k.shape[0], w_k.shape[1]
    rope = 2 * cos_part.shape[1]
    whole = lambda x: pl.BlockSpec(x.shape, lambda i: (0,) * x.ndim)
    picked = lambda x: pl.BlockSpec((1,) + x.shape[1:], lambda i: (layer, 0, 0, 0))
    outs = [jax.ShapeDtypeStruct((heads, rows, latent), jnp.bfloat16), jax.ShapeDtypeStruct((heads, rows, rope), jnp.bfloat16)]
    return pl.pallas_call(
        query_kernel,
        out_shape=outs,
        grid=(1,),
        in_specs=[whole(c_q), whole(cos_part), whole(sin_part), picked(own_q), picked(peer_q), whole(w_k)],
        out_specs=[whole(outs[0]), whole(outs[1])],
        cost_estimate=pl.CostEstimate(flops=2 * rows * c_q.shape[1] * heads * 192, bytes_accessed=8 * 1024 * 1024, transcendentals=0),
        name='queries',
    )(c_q, cos_part, sin_part, own_q, peer_q, w_k)


def solution(mesh):
    cache_spec = P(None, 'dp', None, None)
    head_spec = P(None, None, 'tp', None)
    weight_specs = (P(), P(), P(), P(), P(), head_spec, head_spec, head_spec, P(None, 'tp', None, None), P(), P(None, None, 'tp'), P(None, None, 'tp'), P(None, 'tp', None))
    in_specs = (P('dp', None), P('dp'), cache_spec, cache_spec) + weight_specs
    out_specs = (P('dp', None), P(None, 'dp', None), P(None, 'dp', None))
    pairs = [(i, i + 1 - 2 * (i % 2)) for i in range(16)]

    def device_body(x_in, pos_ids, ckv_cache, kpe_cache, attn_gain, w_dq, q_gain, w_dkv, kv_gain, w_uq, w_uk, w_uv, w_o, mlp_gain, w_gate, w_up, w_down):
        core, me = ring_place()
        layers, latent = ckv_cache.shape[0], ckv_cache.shape[-1]
        width = x_in.shape[-1]
        nope = w_uk.shape[-1]
        lora = w_dq.shape[-1]
        scale = w_uq.shape[-1] ** -0.5
        first = core * HALF + me * CHUNK
        kpe_t = jnp.swapaxes(kpe_cache, 2, 3)
        gate_t = jnp.swapaxes(w_gate, 1, 2)
        up_t = jnp.swapaxes(w_up, 1, 2)
        w_o_flat = w_o.reshape(layers, -1, width)
        uq_t = jnp.transpose(w_uq, (0, 2, 3, 1))
        uk_t = jnp.transpose(w_uk, (0, 2, 1, 3))
        uv_t = jnp.transpose(w_uv, (0, 2, 1, 3))
        p_uq, p_uk, p_uv = [lax.ppermute(w, 'tp', pairs) for w in (uq_t, uk_t, uv_t)]
        state = lax.dynamic_slice_in_dim(x_in, first, CHUNK, 0)
        pos_rows = lax.dynamic_slice_in_dim(pos_ids, first, CHUNK, 0)
        pos_half = lax.dynamic_slice_in_dim(pos_ids, core * HALF, HALF, 0)
        half_rope = kpe_cache.shape[-1] // 2
        inv_freq = jnp.exp(jnp.arange(half_rope, dtype=jnp.float32) * (-math.log(ROPE_BASE) / half_rope))
        angles = pos_half.astype(jnp.float32)[:, None] * inv_freq
        cos_half, sin_half = jnp.cos(angles), jnp.sin(angles)
        c_rows = []
        k_rows = []
        for layer in range(layers):
            if layer == 0:
                normed = rms_norm(lax.dynamic_slice_in_dim(x_in, core * HALF, HALF, 0), attn_gain[0])
            own_pos = pos_half if layer == 0 else pos_rows
            c_q = rms_norm(jnp.dot(normed, w_dq[layer], preferred_element_type=jnp.float32), q_gain[layer])
            kv_lat = jnp.dot(normed, w_dkv[layer], preferred_element_type=jnp.float32)
            c_new = rms_norm(kv_lat[:, :latent], kv_gain[layer])
            k_new = rotary(kv_lat[:, latent:], own_pos).astype(jnp.bfloat16)
            if layer == 0:
                own_q, c_half, k_half = c_q, c_new, k_new
                rows = jnp.concatenate([c_new, k_new], axis=-1)
                peer_rows = lax.ppermute(rows, 'tp', pairs)
            else:
                pad = jnp.zeros((CHUNK, 192), jnp.bfloat16)
                shard = jnp.concatenate([c_q, c_new, k_new, pad], axis=-1)
                latents, = comm_call(1, False, False, True, False, 2, (shard,), shard.shape[-1])
                own_q = latents[:HALF, :lora]
                c_half, k_half = latents[:HALF, lora:lora + latent], latents[:HALF, lora + latent:lora + latent + 64]
                rows, peer_rows = latents[:HALF, lora:lora + latent + 64], latents[HALF:, lora:lora + latent + 64]
            ordered = jnp.where(core == 0, jnp.concatenate([rows, peer_rows], axis=0), jnp.concatenate([peer_rows, rows], axis=0))
            c_rows.append(ordered[:, :latent])
            k_rows.append(ordered[:, latent:])
            w_k = jnp.concatenate([uk_t[layer], p_uk[layer]], axis=0)
            q_lat, q_rope = query_call(layer, own_q, cos_half, sin_half, uq_t, p_uq, w_k)
            q_lat, q_rope = jnp.transpose(q_lat, (1, 0, 2)), jnp.transpose(q_rope, (1, 0, 2))
            values = jnp.transpose(jnp.concatenate([uv_t[layer], p_uv[layer]], axis=0), (1, 0, 2)).reshape(latent, -1)
            last = layer + 1 == layers
            outs = layer_call(3 + layer, layer, last, pos_ids, q_lat, q_rope, c_half, k_half, values, ckv_cache, kpe_t, state, mlp_gain[layer][None],
                              None if last else attn_gain[layer + 1][None], w_o_flat, gate_t, up_t, w_down, scale)
            if last:
                x_out, = outs
            else:
                state, normed = outs
        return x_out, jnp.stack(c_rows), jnp.stack(k_rows)

    return jax.shard_map(device_body, mesh=mesh, in_specs=in_specs, out_specs=out_specs, check_vma=False)
```

profile of v0, /device:TPU:0, one launch (start us, length us, event | category | flops | bytes accessed | tf_op | source)
XLA Modules:
  0.0 499.9 jit_solution(3545734005730127851)
XLA Ops:
  0.7 3.0 fusion.12
  4.5 1.3 slice_convert_fusion.1
  5.8 1.5 fusion.28
  7.3 7.7 %fusion.8 = f32[256,576]{1,0:T(8,128)S(1)} fusion(bf16[2,7168,576]{1,2,0:T(8,128)(2,1)} %param.24, f32[7168]{0:T(1024)S(1)} %bitcast.96, f32[256]{0:T(256)S(1)} %add_rsqrt_fusion.2, bf16[512,7168]{1,0:T(8,128)(2,1)} %param.17, s32[]{:T(128)S(6)} %select_n.39), kind=kOutput, calls=%fused_computation.10 | convolution fusion | flops 2121269248 | bytes 12547076 | tf_op jit(solution)/shard_map/dot_general | solution.py:607
  15.3 1.3 subtract_convert_fusion
  18.7 11.4 %multiply_reduce_fusion = (f32[256]{0:T(256)S(1)}, f32[256,1536]{1,0:T(8,128)}) fusion(bf16[2,7168,1536]{2,1,0:T(8,128)(2,1)} %param.22, f32[7168]{0:T(1024)S(1)} %bitcast.97, f32[256]{0:T(256)S(1)} %add_rsqrt_fusion.2, bf16[512,7168]{1,0:T(8,128)(2,1)S(1)} %bitcast.93, s32[]{:T(128)S(6)} %select_n.39), kind=kOutput, calls=%fused_computation.20 | convolution fusion | flops 5645271040 | bytes 27293700 | tf_op jit(solution)/shard_map/dot_general | solution.py:606
  30.8 2.5 multiply_convert_fusion.c_ref
  33.3 1.8 constant_dynamic-slice_fusion.refs_6_
  35.2 1.6 slice_bitcast_fusion.3
  37.4 1.3 dynamic-slice_convert_fusion.1
  38.8 1.3 maximum_select_fusion
  41.6 1.6 slice_bitcast_fusion.2
  43.1 1.1 pad_maximum_fusion.1
  44.2 1.3 copy.52
  45.6 1.2 copy.51
  46.8 1.3 slice_bitcast_fusion.4
  48.1 1.5 pad_maximum_fusion
  49.6 9.1 %queries.2 = (bf16[8,256,512]{2,1,0:T(8,128)(2,1)}, bf16[8,256,64]{2,1,0:T(8,128)(2,1)}) custom-call(bf16[256,1536]{1,0:T(8,128)(2,1)} %multiply_convert_fusion.c_ref, f32[256,32]{1,0:T(8,128)} %get-tuple-element.44.cos_ref, f32[256,32]{1,0:T(8,128)} %get-tuple-element.43.sin_ref, bf16[2,4,192,1536]{3,2,1,0:T(8,128)(2,1)} %bitcast.2.own_q, ...), custom_call_target="tpu_custom_call" | custom-call | flops 1207959552 | bytes 8388608 | tf_op jit(solution)/shard_map/queries/pallas_call | solution.py:558
  58.7 4.1 copy.50
  62.8 2.2 copy.55
  65.0 164.8 %layer0.1 = (bf16[32,7168]{1,0:T(8,128)(2,1)}, bf16[32,7168]{1,0:T(8,128)(2,1)}) custom-call(s32[512]{0:T(512)} %refs_0_.3, bf16[256,8,512]{2,1,0:T(8,128)(2,1)} %bitcast.85, bf16[256,8,64]{2,1,0:T(8,128)(2,1)} %bitcast.94, bf16[256,512]{1,0:T(8,128)(2,1)} %copy-done, bf16[256,64]{1,0:T(8,128)(2,1)} %pad_maximum_fusion.7.refs_4_, ...), custom_call_target="tpu_custom_call" | custom-call | tf_op jit(solution)/shard_map/layer0/pallas_call | solution.py:527
  229.8 6.0 %fusion.6 = f32[32,576]{1,0:T(8,128)S(1)} fusion(bf16[32,7168]{1,0:T(8,128)(2,1)} %get-tuple-element.11, bf16[2,7168,576]{1,2,0:T(8,128)(2,1)} %param.24), kind=kOutput, calls=%fused_computation.8 | convolution fusion | flops 264241152 | bytes 8790016 | tf_op jit(solution)/shard_map/dot_general | solution.py:607
  235.8 9.6 %multiply_reduce_fusion.2 = (f32[32]{0:T(128)S(1)}, f32[32,1536]{1,0:T(8,128)S(1)}) fusion(bf16[32,7168]{1,0:T(8,128)(2,1)S(1)} %copy-done.10, bf16[2,7168,1536]{2,1,0:T(8,128)(2,1)} %param.22), kind=kOutput, calls=%fused_computation.48 | convolution fusion | flops 704741376 | bytes 22675584 | tf_op jit(solution)/shard_map/dot_general | solution.py:606
  246.0 25.6 %comm1.1 = bf16[512,2304]{1,0:T(8,128)(2,1)S(1)} custom-call(bf16[32,2304]{1,0:T(8,128)(2,1)S(1)} %concatenate.41.refs_0_), custom_call_target="tpu_custom_call" | custom-call | tf_op jit(solution)/shard_map/comm1/pallas_call | solution.py:181
  273.0 0.9 slice.133.c_ref
  274.2 0.8 slice_bitcast_fusion
  275.0 9.1 %queries.3 = (bf16[8,256,512]{2,1,0:T(8,128)(2,1)}, bf16[8,256,64]{2,1,0:T(8,128)(2,1)}) custom-call(bf16[256,1536]{1,0:T(8,128)(2,1)} %slice.133.c_ref, f32[256,32]{1,0:T(8,128)} %get-tuple-element.44.cos_ref, f32[256,32]{1,0:T(8,128)} %get-tuple-element.43.sin_ref, bf16[2,4,192,1536]{3,2,1,0:T(8,128)(2,1)} %bitcast.2.own_q, ...), custom_call_target="tpu_custom_call" | custom-call | flops 1207959552 | bytes 8388608 | tf_op jit(solution)/shard_map/queries/pallas_call | solution.py:558
  284.1 4.2 copy.49
  289.2 1.1 copy.54
  290.3 200.2 %layer1.1 = bf16[512,7168]{1,0:T(8,128)(2,1)} custom-call(s32[512]{0:T(512)} %refs_0_.3, bf16[256,8,512]{2,1,0:T(8,128)(2,1)} %bitcast.84, bf16[256,8,64]{2,1,0:T(8,128)(2,1)} %bitcast.95, bf16[256,512]{1,0:T(8,128)(2,1)} %slice.136.refs_3_, bf16[256,64]{1,0:T(8,128)(2,1)} %slice.137.refs_4_, bf16[512,1024]{1,0:T(8,128)(2,1)} %bitcast.86, ...), custom_call_target="tpu_custom_call" | custom-call | tf_op jit(solution)/shard_map/layer1/pallas_call | solution.py:527
  490.6 2.3 pad_maximum_fusion.4
  492.8 6.6 %copy.57 = bf16[512,7168]{1,0:T(8,128)(2,1)} copy(bf16[512,7168]{1,0:T(8,128)(2,1)} %layer1.1) | data formatting | bytes 14680064
  (64 shorter events, 9.1 us)
Async XLA Ops:
  0.7 14.6 %copy-start.7 = (f32[32]{0:T(128)}, f32[32]{0:T(128)S(1)}, u32[]{:S(2)}) copy-start(f32[32]{0:T(128)S(1)} %multiply_exponential_fusion) | copy-start | bytes 388
  0.7 18.0 %slice-start = ((s8[7340032]{0:T(1024)(128)(4,1)}), s8[4194304]{0:T(1024)(128)(4,1)S(1)}, s32[]{:S(2)}) async-start(s8[7340032]{0:T(1024)(128)(4,1)} %bitcast.92), calls=%async_computation | async-start | bytes 8388608
  7.3 10.6 %copy-start.1 = (bf16[2,512,4,128]{3,2,1,0:T(4,128)(2,1)S(1)}, bf16[2,512,4,128]{3,2,1,0:T(4,128)(2,1)}, u32[]{:S(2)}) copy-start(bf16[2,512,4,128]{3,2,1,0:T(4,128)(2,1)} %param.27) | copy-start | bytes 3145732
  7.3 11.4 %slice-start.1 = ((s8[7340032]{0:T(1024)(128)(4,1)}), s8[3145728]{0:T(1024)(128)(4,1)S(1)}, s32[]{:S(2)}) async-start(s8[7340032]{0:T(1024)(128)(4,1)} %bitcast.92), calls=%async_computation.1 | async-start | bytes 6291456
  15.3 23.5 %copy-start = (bf16[256,512]{1,0:T(8,128)(2,1)}, bf16[256,512]{1,0:T(8,128)(2,1)S(1)}, u32[]{:S(2)}) copy-start(bf16[256,512]{1,0:T(8,128)(2,1)S(1)} %multiply_convert_fusion.1.refs_3_) | copy-start | bytes 786436
  17.4 21.4 %collective-permute-start.3 = (bf16[256,576]{1,0:T(8,128)(2,1)}, bf16[256,576]{1,0:T(8,128)(2,1)}, u32[]{:S(2)}, u32[]{:S(2)}) collective-permute-start(bf16[256,576]{1,0:T(8,128)(2,1)} %pad_maximum_fusion.5), channel_id=1, source_target_pairs={{0,1},{1,0},{2,3},{3,2},{4,5},{5,4},{6,7},{7,6},{8,9},{9,8},{10,11... | collective-permute-start | bytes 884744 | tf_op jit(solution)/shard_map/ppermute | solution.py:613
  18.1 28.7 %collective-permute-start.1 = (bf16[2,4,512,128]{3,2,1,0:T(8,128)(2,1)S(1)}, bf16[2,4,512,128]{3,2,1,0:T(8,128)(2,1)}, u32[]{:S(2)}, u32[]{:S(2)}) collective-permute-start(bf16[2,4,512,128]{3,2,1,0:T(8,128)(2,1)S(1)} %bitcast.88), channel_id=1, source_target_pairs={{0,1},{1,0},{2,3},{3,2},{4,5},{5,4},{6,7},{7,6},{8,9},{9,8},{10,11... | collective-permute-start | bytes 3145736 | tf_op jit(solution)/shard_map/ppermute | solution.py:592
  18.1 23.4 %collective-permute-start.2 = (bf16[2,4,512,128]{3,1,2,0:T(4,128)(2,1)}, bf16[2,4,512,128]{3,1,2,0:T(4,128)(2,1)}, u32[]{:S(2)}, u32[]{:S(2)}) collective-permute-start(bf16[2,4,512,128]{3,1,2,0:T(4,128)(2,1)} %bitcast.10), channel_id=1, source_target_pairs={{0,1},{1,0},{2,3},{3,2},{4,5},{5,4},{6,7},{7,6},{8,9},{9,8},{10,11... | collective-permute-start | bytes 3145736 | tf_op jit(solution)/shard_map/ppermute | solution.py:592
  18.6 11.5 %copy-start.5 = (bf16[2,1536]{1,0:T(2,128)(2,1)S(1)}, bf16[2,1536]{1,0:T(2,128)(2,1)}, u32[]{:S(2)}) copy-start(bf16[2,1536]{1,0:T(2,128)(2,1)} %param.23) | copy-start | bytes 18436
  18.6 30.9 %collective-permute-start = (bf16[2,4,192,1536]{3,2,1,0:T(8,128)(2,1)}, bf16[2,4,192,1536]{3,2,1,0:T(8,128)(2,1)}, u32[]{:S(2)}, u32[]{:S(2)}) collective-permute-start(bf16[2,4,192,1536]{3,2,1,0:T(8,128)(2,1)} %bitcast.2.own_q), channel_id=1, source_target_pairs={{0,1},{1,0},{2,3},{3,2},{4,5},{5,4},{6,7},{7,6},{8,9},{9,8},{10,11... | collective-permute-start | bytes 14155784 | tf_op jit(solution)/shard_map/ppermute | solution.py:592
  229.8 6.0 %copy-start.10 = (bf16[32,7168]{1,0:T(8,128)(2,1)S(1)}, bf16[32,7168]{1,0:T(8,128)(2,1)}, u32[]{:S(2)}) copy-start(bf16[32,7168]{1,0:T(8,128)(2,1)} %get-tuple-element.11) | copy-start | bytes 1376260
  235.8 9.7 %copy-start.8 = (f32[32]{0:T(128)S(1)}, f32[32]{0:T(128)}, u32[]{:S(2)}) copy-start(f32[32]{0:T(128)} %copy-done.7) | copy-start | bytes 388
  235.8 9.7 %copy-start.9 = (f32[32]{0:T(128)S(1)}, f32[32]{0:T(128)}, u32[]{:S(2)}) copy-start(f32[32]{0:T(128)} %dynamic-slice_convert_fusion.1) | copy-start | bytes 388
  235.8 9.9 %copy-start.6 = (f32[1,512]{1,0:T(1,128)S(1)}, f32[1,512]{1,0:T(1,128)}, u32[]{:S(2)}) copy-start(f32[1,512]{1,0:T(1,128)} %get-tuple-element.41) | copy-start | bytes 6148
  235.8 10.0 %copy-start.4 = (f32[1536]{0:T(1024)S(1)}, f32[1536]{0:T(1024)}, u32[]{:S(2)}) copy-start(f32[1536]{0:T(1024)} %get-tuple-element.21) | copy-start | bytes 18436
  275.0 13.3 %copy-start.3 = (bf16[1,512,64]{2,1,0:T(8,128)(2,1)S(1)}, bf16[1,512,64]{2,1,0:T(8,128)(2,1)}, u32[]{:S(2)}) copy-start(bf16[1,512,64]{2,1,0:T(8,128)(2,1)} %slice_bitcast_fusion.11) | copy-start | bytes 196612
  284.1 5.1 %copy-start.2 = (bf16[8,256,64]{2,1,0:T(8,128)(2,1)S(1)}, bf16[8,256,64]{2,1,0:T(8,128)(2,1)}, u32[]{:S(2)}) copy-start(bf16[8,256,64]{2,1,0:T(8,128)(2,1)} %get-tuple-element.13) | copy-start | bytes 786436
where the time goes:
time: 505 us; the launch traced here: 500 us
  Pallas kernels  409 us (81%)
  matrix products  34.6 us (7%)
  local copies, waits for them, and re-layouts  32.9 us (7%)
  other arithmetic  20.9 us (4%)
    pallas_call x2, Pallas kernels, layer_call(): pl.pallas_call(functools.partial(layer_kernel, layer, last, subs, scale),...  365 us
    pallas_call x1, Pallas kernels, comm_call(): pl.pallas_call(functools.partial(comm_kernel, reduce, norm, gather, canon...  25.6 us
    dot_general x2, matrix products, device_body(): jnp.dot(normed, w_dq[layer], preferred_element_type=jnp.float32)  20.9 us
    pallas_call x2, Pallas kernels, query_call(): pl.pallas_call(query_kernel, out_shape=outs, grid=(1,), in_specs=[whole(c...  18.2 us
    dot_general x2, matrix products, device_body(): kv_lat = jnp.dot(normed, w_dkv[layer], preferred_element_type=jnp.float32)  13.7 us
    pallas_call x4, local copies, waits for them, and re-layouts, query_call(): pl.pallas_call(query_kernel, out_shape=outs, grid=(1,), in_specs=[whole(c...  11.6 us
    unnamed x31, local copies, waits for them, and re-layouts  10.2 us
  transfers between devices with their start and end apart: 4, of which 0 were waited for; matrix products, arithmetic and copies ran while one was open for 6% of the time, Pallas kernels for 0%

commit v1 on v0

--- a/solution.py
+++ b/solution.py
@@ -48,145 +48,56 @@
     return (z * 2 + y) * 2 + core
 
 
-def comm_kernel(reduce, norm, gather, canonical, subs, *refs):
-    refs = list(refs)
-    if reduce:
-        part_ref = refs.pop(0)
-        hidden_ref = refs.pop(0)
-        gain_ref = refs.pop(0) if norm else None
-        state_ref = refs.pop(0) if norm else None
-        normed_ref = refs.pop(0) if norm and not gather else None
-    else:
-        shard_ref = refs.pop(0)
-    full_ref = refs.pop(0) if gather else None
-    if reduce:
-        pair_buf, recv_buf, send_buf, pair_send, pair_recv, rs_send, rs_recv = refs[:7]
-        refs = refs[7:]
-    if gather:
-        ag_send, ag_recv, fw_send, fw_recv = refs[:4]
+def gather_kernel(shard_ref, full_ref, ag_send, ag_recv, fw_send, fw_recv):
     core, me = ring_place()
     dp_index = lax.axis_index('dp')
     right = (dp_index, ring_device((me + 1) % RING, core))
     left = (dp_index, ring_device((me + RING - 1) % RING, core))
     peer = (dp_index, ring_device(me, 1 - core))
-    width = (part_ref if reduce else shard_ref).shape[-1]
-    cols = width // subs
-
     barrier = pltpu.get_barrier_semaphore()
     for other in (left, right, peer):
         pl.semaphore_signal(barrier, inc=1, device_id=other, device_id_type=MESH)
+    full_ref[pl.ds(pl.multiple_of(me * CHUNK, CHUNK), CHUNK), :] = shard_ref[...]
     pl.semaphore_wait(barrier, 3)
-
-    def remote(src, dst, send, recv, target):
-        copy = pltpu.make_async_remote_copy(src_ref=src, dst_ref=dst, send_sem=send, recv_sem=recv, device_id=target, device_id_type=MESH)
-        copy.start()
-        return copy
-
-    pending = []
-    ways = ((right, -1), (left, 1))
-    if reduce:
-        pair_copies = {}
-        for step in range(RING):
-            for way, (target, sign) in enumerate(ways):
-                piece = step * 2 + way
-                chunk = (me + RING + sign * (1 + step)) % RING
-                row = pl.multiple_of(chunk * CHUNK + way * PIECE, PIECE)
-                pair_copies[piece] = remote(part_ref.at[pl.ds(HALF + row, PIECE)], pair_buf.at[piece], pair_send.at[piece], pair_recv.at[piece], peer)
-        ring_copies = {}
-        for step in range(RING):
-            for way, (target, sign) in enumerate(ways):
-                piece = step * 2 + way
-                chunk = (me + RING + sign * (1 + step)) % RING
-                row = pl.multiple_of(chunk * CHUNK + way * PIECE, PIECE)
-                pair_copies[piece].wait()
-                for sub in range(subs):
-                    span = pl.ds(sub * cols, cols)
-                    total = part_ref[pl.ds(row, PIECE), span].astype(jnp.float32) + pair_buf[piece, :, span].astype(jnp.float32)
-                    if step > 0:
-                        before = ring_copies[step - 1, way, sub]
-                        before.wait_recv()
-                        pending.append(before)
-                        total = total + recv_buf[(step - 1) * 2 + way, :, span].astype(jnp.float32)
-                    if step < RING - 1:
-                        send_buf[piece, :, span] = total.astype(jnp.bfloat16)
-                        ring_copies[step, way, sub] = remote(send_buf.at[piece, :, span], recv_buf.at[piece, :, span], rs_send.at[piece * subs + sub], rs_recv.at[piece * subs + sub], target)
-                    else:
-                        rows = pl.ds(way * PIECE, PIECE)
-                        mixed = (hidden_ref[rows, span].astype(jnp.float32) + total).astype(jnp.bfloat16)
-                        if norm:
-                            state_ref[rows, span] = mixed
-                        else:
-                            own = pl.multiple_of((core * HALF if canonical else 0) + me * CHUNK + way * PIECE, PIECE)
-                            full_ref[pl.ds(own, PIECE), span] = mixed
-        if norm:
-            for way in range(2):
-                rows = pl.ds(way * PIECE, PIECE)
-                values = state_ref[rows, :].astype(jnp.float32)
-                inv_rms = lax.rsqrt(jnp.mean(values * values, axis=-1, keepdims=True) + NORM_EPS)
-                normed = (values * inv_rms * gain_ref[...].astype(jnp.float32)).astype(jnp.bfloat16)
-                if gather:
-                    own = pl.multiple_of((core * HALF if canonical else 0) + me * CHUNK + way * PIECE, PIECE)
-                    full_ref[pl.ds(own, PIECE), :] = normed
-                else:
-                    normed_ref[rows, :] = normed
-    elif gather:
-        own = pl.multiple_of((core * HALF if canonical else 0) + me * CHUNK, PIECE)
-        full_ref[pl.ds(own, CHUNK), :] = shard_ref[...]
-    if gather:
-        base_here = core * HALF if canonical else 0
-        base_peer = core * HALF if canonical else HALF
-
-        def place(base, chunk, way):
-            return pl.ds(pl.multiple_of(base + chunk * CHUNK + way * PIECE, PIECE), PIECE)
-
-        ring_copies = {}
-        fw_copies = []
-        for step in range(RING):
-            for way, (target, sign) in enumerate(ways):
+    ring = {}
+    handed = []
+    for step in range(5):
+        for sub in range(2):
+            for way, (target, sign, limit) in enumerate(((right, -1, 4), (left, 1, 3))):
+                if step > limit:
+                    continue
                 chunk = (me + RING + sign * step) % RING
-                here = place(base_here, chunk, way)
-                there = place(base_peer, chunk, way)
-                for sub in range(subs):
-                    span = pl.ds(sub * cols, cols)
-                    slot = (step * 2 + way) * subs + sub
-                    if step > 0:
-                        before = ring_copies[step - 1, way, sub]
-                        before.wait_recv()
-                        pending.append(before)
-                    if step < RING - 1:
-                        ring_copies[step, way, sub] = remote(full_ref.at[here, span], full_ref.at[here, span], ag_send.at[slot], ag_recv.at[slot], target)
-                    fw_copies.append(remote(full_ref.at[here, span], full_ref.at[there, span], fw_send.at[slot], fw_recv.at[slot], peer))
-        for copy in fw_copies:
-            copy.wait()
-    for copy in pending:
+                row = pl.multiple_of(chunk * CHUNK + sub * PIECE, PIECE)
+                here = full_ref.at[pl.ds(row, PIECE)]
+                slot = (step * 2 + way) * 2 + sub
+                if step > 0:
+                    ring[step - 1, way, sub].wait_recv()
+                if step < limit:
+                    ring[step, way, sub] = pltpu.make_async_remote_copy(src_ref=here, dst_ref=here, send_sem=ag_send.at[slot], recv_sem=ag_recv.at[slot], device_id=target, device_id_type=MESH)
+                    ring[step, way, sub].start()
+                if step > 0 or way == 0:
+                    there = full_ref.at[pl.ds(pl.multiple_of(HALF + row, PIECE), PIECE)]
+                    copy = pltpu.make_async_remote_copy(src_ref=here, dst_ref=there, send_sem=fw_send.at[slot], recv_sem=fw_recv.at[slot], device_id=peer, device_id_type=MESH)
+                    copy.start()
+                    handed.append(copy)
+    for copy in handed:
+        copy.wait()
+    for copy in ring.values():
         copy.wait_send()
 
 
-def comm_call(call_id, reduce, norm, gather, canonical, subs, operands, width):
+def gather_call(shard):
     vmem = pl.BlockSpec(memory_space=pltpu.VMEM)
-    outs = []
-    if reduce and norm:
-        outs.append(jax.ShapeDtypeStruct((CHUNK, width), jnp.bfloat16))
-        if not gather:
-            outs.append(jax.ShapeDtypeStruct((CHUNK, width), jnp.bfloat16))
-    if gather:
-        outs.append(jax.ShapeDtypeStruct((2 * HALF, width), jnp.bfloat16))
-    scratch = []
     dma = pltpu.SemaphoreType.DMA
-    if reduce:
-        scratch += [pltpu.VMEM((16, PIECE, width), jnp.bfloat16), pltpu.VMEM((14, PIECE, width), jnp.bfloat16), pltpu.VMEM((14, PIECE, width), jnp.bfloat16)]
-        scratch += [dma((16,)), dma((16,)), dma((14 * subs,)), dma((14 * subs,))]
-    if gather:
-        scratch += [dma((14 * subs,)), dma((14 * subs,)), dma((16 * subs,)), dma((16 * subs,))]
     return pl.pallas_call(
-        functools.partial(comm_kernel, reduce, norm, gather, canonical, subs),
-        out_shape=outs,
-        in_specs=[vmem] * len(operands),
-        out_specs=[vmem] * len(outs),
-        scratch_shapes=scratch,
-        compiler_params=pltpu.CompilerParams(collective_id=call_id, has_side_effects=True, vmem_limit_bytes=48 * 1024 * 1024),
-        name='comm%d' % call_id,
-    )(*operands)
+        gather_kernel,
+        out_shape=jax.ShapeDtypeStruct((2 * HALF, shard.shape[-1]), shard.dtype),
+        in_specs=[vmem],
+        out_specs=vmem,
+        scratch_shapes=[dma((16,)), dma((16,)), dma((20,)), dma((20,))],
+        compiler_params=pltpu.CompilerParams(collective_id=1, has_side_effects=True, vmem_limit_bytes=8 * 1024 * 1024),
+        name='gather',
+    )(shard)
 
 
 def layer_kernel(layer, last, subs, scale, *refs):
@@ -201,7 +112,7 @@
     else:
         state_out, normed_out, b_full = refs[:3]
         refs = refs[3:]
-    (ckv, kpe, o_own, o_out, o_in, wo, gate, up, down, batch, act, state, own_part, pair_out, pair_buf, recv_buf, send_buf,
+    (ckv, kpe, o_own, o_out, o_in, wo, gate, up, down, batch, gate_pre, up_pre, act, state, own_part, pair_out, pair_buf, recv_buf, send_buf,
      ckv_sem, kpe_sem, o_send, o_recv, w_sem, pair_send, pair_recv, rs_send, rs_recv, ag_send, ag_recv, fw_send, fw_recv) = refs
     width = hidden_ref.shape[-1]
     cols = width // subs
@@ -316,16 +227,18 @@
         return remote(send_buf.at[where], recv_buf.at[where], rs_send.at[slot], rs_recv.at[slot], ways[way][0])
 
     def reduce_scatter(attention, weight, ready, finish):
-        def multiply(step):
+        per_sub = -(-blocks // subs)
+
+        def multiply(step, sub):
             if attention:
-                o_copy(step).wait_recv()
+                if sub == 0:
+                    o_copy(step).wait_recv()
                 lhs = jnp.concatenate([o_own[step], o_in[step]], axis=0)
             else:
                 near, far = piece_row(step + 1, 0), piece_row(step + 1, 1)
                 lhs = jnp.concatenate([act[pl.ds(pl.multiple_of(base + at, PIECE), PIECE), :] for base in (0, HALF) for at in (near, far)], axis=0)
-
-            def one_block(i, carry):
-                span = pl.ds(pl.multiple_of(i * block, block), block)
+            for i in range(sub * per_sub, min((sub + 1) * per_sub, blocks)):
+                span = pl.ds(i * block, block)
                 if ready is not None:
                     @pl.when(step == 0)
                     def _():
@@ -333,58 +246,50 @@
                 prod = jnp.dot(lhs, weight[:, span], preferred_element_type=jnp.float32)
                 own_part[step % 2, :, span] = prod[:CHUNK]
                 pair_out[step, :, span] = prod[CHUNK:].astype(jnp.bfloat16)
-                return carry
-
-            lax.fori_loop(0, blocks, one_block, 0)
-            pair_copy(step).start()
-
-        def pass_on(step):
-            pair_copy(step).wait_recv()
-            for sub in range(subs):
-                span = pl.ds(sub * cols, cols)
-                for way in range(2):
-                    rows = pl.ds(way * PIECE, PIECE)
-
-                    @pl.when(step > 0)
-                    def _():
-                        rs_copy(step - 1, way, sub).wait_recv()
-                        own_part[step % 2, rows, span] += recv_buf[step - 1, rows, span].astype(jnp.float32)
-
-                    total = own_part[step % 2, rows, span] + pair_buf[step, rows, span].astype(jnp.float32)
-
-                    @pl.when(step < RING - 1)
-                    def _():
-                        send_buf[step, rows, span] = total.astype(jnp.bfloat16)
-                        rs_copy(step, way, sub).start()
-
-                    @pl.when(step == RING - 1)
-                    def _():
-                        finish(rows, span, total)
+            if sub == subs - 1:
+                pair_copy(step).start()
+
+        def pass_on(step, sub):
+            if sub == 0:
+                pair_copy(step).wait_recv()
+            span = pl.ds(sub * cols, cols)
+            for way in range(2):
+                rows = pl.ds(way * PIECE, PIECE)
+
+                @pl.when(step > 0)
+                def _():
+                    rs_copy(step - 1, way, sub).wait_recv()
+                    own_part[step % 2, rows, span] += recv_buf[step - 1, rows, span].astype(jnp.float32)
+
+                total = own_part[step % 2, rows, span] + pair_buf[step, rows, span].astype(jnp.float32)
+
+                @pl.when(step < RING - 1)
+                def _():
+                    send_buf[step, rows, span] = total.astype(jnp.bfloat16)
+                    rs_copy(step, way, sub).start()
+
+                @pl.when(step == RING - 1)
+                def _():
+                    finish(rows, span, total)
+
+        lag = 1 if attention else 0
 
         def staggered(i, carry):
             if attention:
                 @pl.when(i < RING)
                 def _():
                     attend(i)
-
-                @pl.when(i > 1)
+            for sub in range(subs):
+                @pl.when((i >= lag) & (i < RING + lag))
                 def _():
-                    pass_on(i - 2)
-
-                @pl.when((i > 0) & (i <= RING))
+                    multiply(i - lag, sub)
+
+                @pl.when(i > lag)
                 def _():
-                    multiply(i - 1)
-            else:
-                @pl.when(i < RING)
-                def _():
-                    multiply(i)
-
-                @pl.when(i > 0)
-                def _():
-                    pass_on(i - 1)
+                    pass_on(i - lag - 1, sub)
             return carry
 
-        lax.fori_loop(0, RING + (2 if attention else 1), staggered, 0)
+        lax.fori_loop(0, RING + 1 + lag, staggered, 0)
         if attention:
             for k in range(quarters):
                 for copy in cache_copies(0, k):
@@ -428,30 +333,41 @@
                     for way in range(2):
                         if odd:
                             ag_copy(step - 1, way, sub).wait_recv()
+
+                            @pl.when(pair < RING // 2 - 1)
+                            def _():
+                                ag_copy(step, way, sub).start()
                         else:
                             @pl.when(pair > 0)
                             def _():
                                 ag_copy(step - 1, way, sub).wait_recv()
-                        if odd:
-                            @pl.when(pair < RING // 2 - 1)
-                            def _():
-                                ag_copy(step, way, sub).start()
-                        else:
+
                             ag_copy(step, way, sub).start()
                         fw_copy(step, way, sub).start()
-            for odd in range(2):
-                for way in range(2):
-                    for sub in range(subs):
-                        fw_copy(pair * 2 + odd, way, sub).wait_recv()
-            if consume is not None:
-                consume(pair)
+                    if consume is not None and sub % 2:
+                        @pl.when(pair > 0)
+                        def _():
+                            do_part(pair - 1, odd * 2 + sub // 2)
             return carry
 
+        def do_part(pair, part):
+            if part == 0:
+                for odd in range(2):
+                    for way in range(2):
+                        for sub in range(subs):
+                            fw_copy(pair * 2 + odd, way, sub).wait_recv()
+            consume(pair, part)
+
         lax.fori_loop(0, RING // 2, two_steps, 0)
+        if consume is not None:
+            for part in range(4):
+                do_part(RING // 2 - 1, part)
 
         def drain(step, carry):
             for way in range(2):
                 for sub in range(subs):
+                    if consume is None:
+                        fw_copy(step, way, sub).wait_recv()
                     fw_copy(step, way, sub).wait_send()
 
                     @pl.when(step < RING - 1)
@@ -471,20 +387,24 @@
     up_copy.wait()
     down_copy.wait()
 
-    def mlp_rows(pair):
+    def mlp_rows(pair, part):
         places = [(base, step, way) for base in (0, HALF) for step in range(2) for way in range(2)]
-        for i, (base, odd, way) in enumerate(places):
-            at = pl.multiple_of(base + piece_row(pair * 2 + odd, way), PIECE)
-            batch[pl.ds(i * PIECE, PIECE), :] = b_full[pl.ds(at, PIECE), :]
         dims = (((1,), (1,)), ((), ()))
-        gate_pre = lax.dot_general(gate[...], batch[...], dims, preferred_element_type=jnp.float32)
-        up_pre = lax.dot_general(up[...], batch[...], dims, preferred_element_type=jnp.float32)
-        hidden_act = jax.nn.silu(gate_pre) * up_pre
-        padded = jnp.concatenate([hidden_act, jnp.zeros((act.shape[1] - ffn, 128), jnp.float32)], axis=0)
-        turned = jnp.transpose(padded).astype(jnp.bfloat16)
-        for i, (base, odd, way) in enumerate(places):
-            at = pl.multiple_of(base + piece_row(pair * 2 + odd, way), PIECE)
-            act[pl.ds(at, PIECE), :] = turned[i * PIECE:(i + 1) * PIECE]
+        if part == 0:
+            for i, (base, odd, way) in enumerate(places):
+                at = pl.multiple_of(base + piece_row(pair * 2 + odd, way), PIECE)
+                batch[pl.ds(i * PIECE, PIECE), :] = b_full[pl.ds(at, PIECE), :]
+        elif part == 1:
+            gate_pre[...] = lax.dot_general(gate[...], batch[...], dims, preferred_element_type=jnp.float32)
+        elif part == 2:
+            up_pre[...] = lax.dot_general(up[...], batch[...], dims, preferred_element_type=jnp.float32)
+        else:
+            hidden_act = jax.nn.silu(gate_pre[...]) * up_pre[...]
+            padded = jnp.concatenate([hidden_act, jnp.zeros((act.shape[1] - ffn, 128), jnp.float32)], axis=0)
+            turned = jnp.transpose(padded).astype(jnp.bfloat16)
+            for i, (base, odd, way) in enumerate(places):
+                at = pl.multiple_of(base + piece_row(pair * 2 + odd, way), PIECE)
+                act[pl.ds(at, PIECE), :] = turned[i * PIECE:(i + 1) * PIECE]
 
     all_gather(b_full, 0, HALF, mlp_rows)
 
@@ -520,7 +440,7 @@
     mine = w_o.shape[1]
     scratch = ([] if last else [bf(2 * HALF, width)]) + [
         bf(quarters, seqs, *ckv_cache.shape[2:]), bf(quarters, seqs, *kpe_cache.shape[2:]), bf(RING, CHUNK, mine), bf(RING, CHUNK, mine), bf(RING, CHUNK, mine),
-        bf(mine, width), bf(ffn, width), bf(ffn, width), bf(padded, width), bf(128, width), bf(2 * HALF, padded),
+        bf(mine, width), bf(ffn, width), bf(ffn, width), bf(padded, width), bf(128, width), pltpu.VMEM((ffn, 128), jnp.float32), pltpu.VMEM((ffn, 128), jnp.float32), bf(2 * HALF, padded),
         bf(CHUNK, width), pltpu.VMEM((2, CHUNK, width), jnp.float32), bf(RING, CHUNK, width), bf(RING, CHUNK, width), bf(RING - 1, CHUNK, width), bf(RING - 1, CHUNK, width),
         dma((quarters,)), dma((quarters,)), dma((RING,)), dma((RING,)), dma((10,)), dma((RING,)), dma((RING,)),
         dma((14 * subs,)), dma((14 * subs,)), dma((14 * subs,)), dma((14 * subs,)), dma((16 * subs,)), dma((16 * subs,))]
@@ -561,6 +481,7 @@
         grid=(1,),
         in_specs=[whole(c_q), whole(cos_part), whole(sin_part), picked(own_q), picked(peer_q), whole(w_k)],
         out_specs=[whole(outs[0]), whole(outs[1])],
+        compiler_params=pltpu.CompilerParams(vmem_limit_bytes=28 * 1024 * 1024),
         cost_estimate=pl.CostEstimate(flops=2 * rows * c_q.shape[1] * heads * 192, bytes_accessed=8 * 1024 * 1024, transcendentals=0),
         name='queries',
     )(c_q, cos_part, sin_part, own_q, peer_q, w_k)
@@ -601,7 +522,7 @@
         k_rows = []
         for layer in range(layers):
             if layer == 0:
-                normed = rms_norm(lax.dynamic_slice_in_dim(x_in, core * HALF, HALF, 0), attn_gain[0])
+                normed = lax.optimization_barrier(rms_norm(lax.dynamic_slice_in_dim(x_in, core * HALF, HALF, 0), attn_gain[0]))
             own_pos = pos_half if layer == 0 else pos_rows
             c_q = rms_norm(jnp.dot(normed, w_dq[layer], preferred_element_type=jnp.float32), q_gain[layer])
             kv_lat = jnp.dot(normed, w_dkv[layer], preferred_element_type=jnp.float32)
@@ -612,9 +533,9 @@
                 rows = jnp.concatenate([c_new, k_new], axis=-1)
                 peer_rows = lax.ppermute(rows, 'tp', pairs)
             else:
-                pad = jnp.zeros((CHUNK, 192), jnp.bfloat16)
+                pad = jnp.zeros((CHUNK, 64), jnp.bfloat16)
                 shard = jnp.concatenate([c_q, c_new, k_new, pad], axis=-1)
-                latents, = comm_call(1, False, False, True, False, 2, (shard,), shard.shape[-1])
+                latents = gather_call(shard)
                 own_q = latents[:HALF, :lora]
                 c_half, k_half = latents[:HALF, lora:lora + latent], latents[:HALF, lora + latent:lora + latent + 64]
                 rows, peer_rows = latents[:HALF, lora:lora + latent + 64], latents[HALF:, lora:lora + latent + 64]

time: 505 us -> 481 us (0.952)
  Pallas kernels: 409 us -> 392 us
    pallas_call x1, Pallas kernels: 25.6 us -> 18.6 us  [gather_call(): pl.pallas_call(gather_kernel, out_shape=jax.ShapeDtypeStruct((2 * HALF, s...]
    pallas_call x2, Pallas kernels: 365 us -> 359 us  [layer_call(): pl.pallas_call(functools.partial(layer_kernel, layer, last, subs, scale),...]
    unnamed x31 -> x45, local copies, waits for them, and re-layouts: 10.2 us -> 11.5 us
  transfers between devices with their start and end apart: 4 -> 4, of which waited for: 0 -> 0; matrix products, arithmetic and copies ran while one was open for 6% -> 9% of each run, Pallas kernels for 0% -> 0%
where the time goes in v1:
time: 481 us; the launch traced here: 476 us
  Pallas kernels  392 us (81%)
  matrix products  32.4 us (7%)
  local copies, waits for them, and re-layouts  30 us (6%)
  other arithmetic  19.1 us (4%)
    pallas_call x2, Pallas kernels, layer_call(): pl.pallas_call(functools.partial(layer_kernel, layer, last, subs, scale),...  359 us
    dot_general x2, matrix products, device_body(): jnp.dot(normed, w_dq[layer], preferred_element_type=jnp.float32)  20.9 us
    pallas_call x1, Pallas kernels, gather_call(): pl.pallas_call(gather_kernel, out_shape=jax.ShapeDtypeStruct((2 * HALF, s...  18.6 us
    pallas_call x2, Pallas kernels, query_call(): pl.pallas_call(query_kernel, out_shape=outs, grid=(1,), in_specs=[whole(c...  14.2 us
    unnamed x45, local copies, waits for them, and re-layouts  11.5 us
    dot_general x2, matrix products, device_body(): kv_lat = jnp.dot(normed, w_dkv[layer], preferred_element_type=jnp.float32)  11.4 us
  transfers between devices with their start and end apart: 4, of which 0 were waited for; matrix products, arithmetic and copies ran while one was open for 9% of the time, Pallas kernels for 0%

profile of v1, /device:TPU:0, one launch (start us, length us, event | category | flops | bytes accessed | tf_op | source)
XLA Modules:
  0.0 475.9 jit_solution(2775428293448658968)
XLA Ops:
  0.7 1.4 copy.53
  2.8 2.9 fusion.12
  7.0 3.1 fusion.14
  10.0 5.4 %fusion.8 = f32[256,576]{1,0:T(8,128)S(1)} fusion(bf16[256,7168]{1,0:T(8,128)(2,1)S(1)} %fusion.14, bf16[2,7168,576]{1,2,0:T(8,128)(2,1)} %param.24), kind=kOutput, calls=%fused_computation.10 | convolution fusion | flops 2113929216 | bytes 12517376 | tf_op jit(solution)/shard_map/dot_general | solution.py:528
  16.4 0.8 pad_maximum_fusion.5
  17.7 11.6 %multiply_reduce_fusion = (f32[256]{0:T(256)S(1)}, f32[256,1536]{1,0:T(8,128)}) fusion(bf16[256,7168]{1,0:T(8,128)(2,1)S(1)} %fusion.14, bf16[2,7168,1536]{2,1,0:T(8,128)(2,1)} %param.22), kind=kOutput, calls=%fused_computation.20 | convolution fusion | flops 5637931008 | bytes 27264000 | tf_op jit(solution)/shard_map/dot_general | solution.py:527
  30.1 1.6 multiply_convert_fusion.c_ref
  31.7 1.8 constant_dynamic-slice_fusion.refs_6_
  33.6 2.5 slice_bitcast_fusion.3
  37.5 1.4 maximum_select_fusion
  39.6 0.9 slice_bitcast_fusion.1
  40.5 1.6 slice_bitcast_fusion.2
  42.1 1.1 pad_maximum_fusion.1
  43.2 1.3 copy.52
  44.4 1.3 copy.51
  45.8 1.3 slice_bitcast_fusion.4
  47.0 1.2 pad_maximum_fusion
  48.2 7.1 %queries.2 = (bf16[8,256,512]{2,1,0:T(8,128)(2,1)S(1)}, bf16[8,256,64]{2,1,0:T(8,128)(2,1)S(1)}) custom-call(bf16[256,1536]{1,0:T(8,128)(2,1)S(1)} %multiply_convert_fusion.c_ref, f32[256,32]{1,0:T(8,128)S(1)} %get-tuple-element.44.cos_ref, f32[256,32]{1,0:T(8,128)S(1)} %get-tuple-element.43.sin_ref, bf16[2,4,192,1536]{3,2,1,0:T(8,128)(2,1)} %bitcast.2.own_q, ...), custom_call_target="tpu_custom_call" | custom-call | flops 1207959552 | bytes 8388608 | tf_op jit(solution)/shard_map/queries/pallas_call | solution.py:478
  55.3 2.5 copy.50
  57.8 1.1 copy.55
  58.9 161.3 %layer0.1 = (bf16[32,7168]{1,0:T(8,128)(2,1)}, bf16[32,7168]{1,0:T(8,128)(2,1)}) custom-call(s32[512]{0:T(512)} %refs_0_.3, bf16[256,8,512]{2,1,0:T(8,128)(2,1)} %bitcast.87, bf16[256,8,64]{2,1,0:T(8,128)(2,1)} %bitcast.94, bf16[256,512]{1,0:T(8,128)(2,1)} %copy-done.5, bf16[256,64]{1,0:T(8,128)(2,1)} %pad_maximum_fusion.7.refs_4_, ...), custom_call_target="tpu_custom_call" | custom-call | tf_op jit(solution)/shard_map/layer0/pallas_call | solution.py:447
  220.2 6.0 %fusion.6 = f32[32,576]{1,0:T(8,128)S(1)} fusion(bf16[32,7168]{1,0:T(8,128)(2,1)} %get-tuple-element.11, bf16[2,7168,576]{1,2,0:T(8,128)(2,1)} %param.24), kind=kOutput, calls=%fused_computation.8 | convolution fusion | flops 264241152 | bytes 8790016 | tf_op jit(solution)/shard_map/dot_general | solution.py:528
  226.3 9.3 %multiply_reduce_fusion.2 = (f32[32]{0:T(128)S(1)}, f32[32,1536]{1,0:T(8,128)S(1)}) fusion(bf16[32,7168]{1,0:T(8,128)(2,1)S(1)} %copy-done.19, bf16[2,7168,1536]{2,1,0:T(8,128)(2,1)} %param.22), kind=kOutput, calls=%fused_computation.48 | convolution fusion | flops 704741376 | bytes 22675584 | tf_op jit(solution)/shard_map/dot_general | solution.py:527
  236.2 18.6 %gather.1 = bf16[512,2176]{1,0:T(8,128)(2,1)S(1)} custom-call(bf16[32,2176]{1,0:T(8,128)(2,1)S(1)} %concatenate.41.shard_ref), custom_call_target="tpu_custom_call" | custom-call | tf_op jit(solution)/shard_map/gather/pallas_call | solution.py:92
  256.5 0.9 slice_bitcast_fusion
  257.4 7.1 %queries.3 = (bf16[8,256,512]{2,1,0:T(8,128)(2,1)S(1)}, bf16[8,256,64]{2,1,0:T(8,128)(2,1)S(1)}) custom-call(bf16[256,1536]{1,0:T(8,128)(2,1)S(1)} %slice.133.c_ref, f32[256,32]{1,0:T(8,128)S(1)} %copy-done.4, f32[256,32]{1,0:T(8,128)S(1)} %copy-done.2, bf16[2,4,192,1536]{3,2,1,0:T(8,128)(2,1)} %bitcast.2.own_q, ...), custom_call_target="tpu_custom_call" | custom-call | flops 1207959552 | bytes 8388608 | tf_op jit(solution)/shard_map/queries/pallas_call | solution.py:478
  264.5 2.5 copy.49
  267.0 0.8 copy.38
  267.8 1.1 copy.54
  268.9 197.7 %layer1.1 = bf16[512,7168]{1,0:T(8,128)(2,1)} custom-call(s32[512]{0:T(512)} %refs_0_.3, bf16[256,8,512]{2,1,0:T(8,128)(2,1)} %bitcast.86, bf16[256,8,64]{2,1,0:T(8,128)(2,1)} %bitcast.95, bf16[256,512]{1,0:T(8,128)(2,1)} %slice.136.refs_3_, bf16[256,64]{1,0:T(8,128)(2,1)} %slice.137.refs_4_, bf16[512,1024]{1,0:T(8,128)(2,1)} %bitcast.88, ...), custom_call_target="tpu_custom_call" | custom-call | tf_op jit(solution)/shard_map/layer1/pallas_call | solution.py:447
  466.6 2.3 pad_maximum_fusion.4
  468.9 6.6 %copy.57 = bf16[512,7168]{1,0:T(8,128)(2,1)} copy(bf16[512,7168]{1,0:T(8,128)(2,1)} %layer1.1) | data formatting | bytes 14680064
  (78 shorter events, 8.4 us)
Async XLA Ops:
  0.6 5.0 %copy-start.13 = (s32[512]{0:T(512)S(1)}, s32[512]{0:T(512)}, u32[]{:S(2)}) copy-start(s32[512]{0:T(512)} %refs_0_.3) | copy-start | bytes 6148
  0.6 5.1 %copy-start.14 = (bf16[2,512]{1,0:T(2,128)(2,1)S(1)}, bf16[2,512]{1,0:T(2,128)(2,1)}, u32[]{:S(2)}) copy-start(bf16[2,512]{1,0:T(2,128)(2,1)} %param.25) | copy-start | bytes 6148
  0.7 5.6 %copy-start.9 = (bf16[2,7168]{1,0:T(2,128)(2,1)S(1)}, bf16[2,7168]{1,0:T(2,128)(2,1)}, u32[]{:S(2)}) copy-start(bf16[2,7168]{1,0:T(2,128)(2,1)} %param.30) | copy-start | bytes 86020
  0.7 5.6 %copy-start.10 = (bf16[2,7168]{1,0:T(2,128)(2,1)S(1)}, bf16[2,7168]{1,0:T(2,128)(2,1)}, u32[]{:S(2)}) copy-start(bf16[2,7168]{1,0:T(2,128)(2,1)} %param.21) | copy-start | bytes 86020
  2.1 43.7 %collective-permute-start.1 = (bf16[2,4,512,128]{3,2,1,0:T(8,128)(2,1)S(1)}, bf16[2,4,512,128]{3,2,1,0:T(8,128)(2,1)}, u32[]{:S(2)}, u32[]{:S(2)}) collective-permute-start(bf16[2,4,512,128]{3,2,1,0:T(8,128)(2,1)S(1)} %bitcast.90), channel_id=1, source_target_pairs={{0,1},{1,0},{2,3},{3,2},{4,5},{5,4},{6,7},{7,6},{8,9},{9,8},{10,11... | collective-permute-start | bytes 3145736 | tf_op jit(solution)/shard_map/ppermute | solution.py:513
  2.6 37.8 %collective-permute-start.2 = (bf16[2,4,512,128]{3,1,2,0:T(4,128)(2,1)}, bf16[2,4,512,128]{3,1,2,0:T(4,128)(2,1)}, u32[]{:S(2)}, u32[]{:S(2)}) collective-permute-start(bf16[2,4,512,128]{3,1,2,0:T(4,128)(2,1)} %bitcast.96), channel_id=1, source_target_pairs={{0,1},{1,0},{2,3},{3,2},{4,5},{5,4},{6,7},{7,6},{8,9},{9,8},{10,11... | collective-permute-start | bytes 3145736 | tf_op jit(solution)/shard_map/ppermute | solution.py:513
  2.7 13.0 %copy-start.16 = (f32[32]{0:T(128)}, f32[32]{0:T(128)S(1)}, u32[]{:S(2)}) copy-start(f32[32]{0:T(128)S(1)} %multiply_exponential_fusion) | copy-start | bytes 388
  15.8 21.8 %copy-start.5 = (bf16[256,512]{1,0:T(8,128)(2,1)}, bf16[256,512]{1,0:T(8,128)(2,1)S(1)}, u32[]{:S(2)}) copy-start(bf16[256,512]{1,0:T(8,128)(2,1)S(1)} %multiply_convert_fusion.1.refs_3_) | copy-start | bytes 786436
  16.4 31.8 %copy-start.1 = (f32[256,32]{1,0:T(8,128)}, f32[256,32]{1,0:T(8,128)S(1)}, u32[]{:S(2)}) copy-start(f32[256,32]{1,0:T(8,128)S(1)} %get-tuple-element.43.sin_ref) | copy-start | bytes 98308
  16.4 31.8 %copy-start.3 = (f32[256,32]{1,0:T(8,128)}, f32[256,32]{1,0:T(8,128)S(1)}, u32[]{:S(2)}) copy-start(f32[256,32]{1,0:T(8,128)S(1)} %get-tuple-element.44.cos_ref) | copy-start | bytes 98308
  17.2 20.3 %collective-permute-start.3 = (bf16[256,576]{1,0:T(8,128)(2,1)}, bf16[256,576]{1,0:T(8,128)(2,1)}, u32[]{:S(2)}, u32[]{:S(2)}) collective-permute-start(bf16[256,576]{1,0:T(8,128)(2,1)} %pad_maximum_fusion.5), channel_id=1, source_target_pairs={{0,1},{1,0},{2,3},{3,2},{4,5},{5,4},{6,7},{7,6},{8,9},{9,8},{10,11... | collective-permute-start | bytes 884744 | tf_op jit(solution)/shard_map/ppermute | solution.py:534
  17.7 11.8 %copy-start.12 = (bf16[2,1536]{1,0:T(2,128)(2,1)S(1)}, bf16[2,1536]{1,0:T(2,128)(2,1)}, u32[]{:S(2)}) copy-start(bf16[2,1536]{1,0:T(2,128)(2,1)} %param.23) | copy-start | bytes 18436
  17.7 30.5 %collective-permute-start = (bf16[2,4,192,1536]{3,2,1,0:T(8,128)(2,1)}, bf16[2,4,192,1536]{3,2,1,0:T(8,128)(2,1)}, u32[]{:S(2)}, u32[]{:S(2)}) collective-permute-start(bf16[2,4,192,1536]{3,2,1,0:T(8,128)(2,1)} %bitcast.2.own_q), channel_id=1, source_target_pairs={{0,1},{1,0},{2,3},{3,2},{4,5},{5,4},{6,7},{7,6},{8,9},{9,8},{10,11... | collective-permute-start | bytes 14155784 | tf_op jit(solution)/shard_map/ppermute | solution.py:513
  37.5 4.5 copy-start.6
  37.5 4.5 copy-start.7
  220.2 6.0 %copy-start.19 = (bf16[32,7168]{1,0:T(8,128)(2,1)S(1)}, bf16[32,7168]{1,0:T(8,128)(2,1)}, u32[]{:S(2)}) copy-start(bf16[32,7168]{1,0:T(8,128)(2,1)} %get-tuple-element.11) | copy-start | bytes 1376260
  226.2 9.5 %copy-start.17 = (f32[32]{0:T(128)S(1)}, f32[32]{0:T(128)}, u32[]{:S(2)}) copy-start(f32[32]{0:T(128)} %copy-done.16) | copy-start | bytes 388
  226.2 9.5 %copy-start.18 = (f32[32]{0:T(128)S(1)}, f32[32]{0:T(128)}, u32[]{:S(2)}) copy-start(f32[32]{0:T(128)} %dynamic-slice_convert_fusion.1) | copy-start | bytes 388
  226.2 9.7 %copy-start.15 = (f32[1,512]{1,0:T(1,128)S(1)}, f32[1,512]{1,0:T(1,128)}, u32[]{:S(2)}) copy-start(f32[1,512]{1,0:T(1,128)} %get-tuple-element.41) | copy-start | bytes 6148
  226.3 9.7 %copy-start.11 = (f32[1536]{0:T(1024)S(1)}, f32[1536]{0:T(1024)}, u32[]{:S(2)}) copy-start(f32[1536]{0:T(1024)} %get-tuple-element.21) | copy-start | bytes 18436
  254.8 2.6 copy-start
  254.8 2.5 copy-start.2
  254.8 2.5 copy-start.4
  264.5 2.5 copy-start.8
